TPU v7x, 8 devices: a whole 2x2x1 slice. The times are simulated.
8 devices in a mesh: data: 8 (over z, y, x, core).
Axes of the slice: x: 2, y: 2, z: 1, core: 2. Of those that a mesh axis runs over, the one named last changes fastest.
Arguments:
- z_one: bfloat16 [512, 256], P('data')
- z_two: bfloat16 [512, 256], P('data')
- protos: bfloat16 [8192, 256], replicated
- queue_one: bfloat16 [2048, 256], P('data')
- queue_two: bfloat16 [2048, 256], P('data')
Outputs:
- output 1: float32 [512, 8192], P('data')
- output 2: float32 [512, 8192], P('data')
- output 3: float32 [], replicated
- output 4: float32 [512, 256], P('data')
- output 5: float32 [512, 256], P('data')
- output 6: float32 [8192, 256], replicated
All inputs are finite; a program needn't handle non-finite values.
Results may differ from a plain program's by a relative error of at most 0.001.
Values are sent between devices in bfloat16 or wider.
A program may use at most 1 GiB of HBM per device.

v0:
```python
import jax
import jax.numpy as jnp
from jax import lax
from jax.sharding import PartitionSpec as P

EPSILON = 0.05
value_a11 = 0.1
value_a14 = 3


def view_codes(own_rows, protos, batch_rows, total_rows):
    protos_count = protos.shape[0]
    scores = jnp.einsum("nd,kd->nk", own_rows, protos, preferred_element_type=jnp.float32)
    transport = jnp.exp(scores / EPSILON)
    for _ in range(value_a14 - 1):
        col_sum = lax.psum(jnp.sum(transport, axis=0), "data")
        transport = transport / (protos_count * col_sum)
        transport = transport / (total_rows * jnp.sum(transport, axis=1, keepdims=True))
    col_sum = lax.psum(jnp.sum(transport, axis=0), "data")
    plan_batch = transport[:batch_rows] / (protos_count * col_sum)
    return plan_batch / jnp.sum(plan_batch, axis=1, keepdims=True), scores[:batch_rows]


def solution(mesh):
    group_size = mesh.shape["data"]

    def local_step(z_one, z_two, protos, queue_one, queue_two):
        batch_rows = z_one.shape[0]
        total_rows = group_size * (batch_rows + queue_one.shape[0])
        batch_total = group_size * batch_rows
        codes_one, score_one = view_codes(jnp.concatenate([z_one, queue_one], axis=0), protos, batch_rows, total_rows)
        codes_two, score_two = view_codes(jnp.concatenate([z_two, queue_two], axis=0), protos, batch_rows, total_rows)
        logp_one = jax.nn.log_softmax(score_one / value_a11, axis=1)
        logp_two = jax.nn.log_softmax(score_two / value_a11, axis=1)
        part_loss = jnp.sum(codes_two * logp_one) + jnp.sum(codes_one * logp_two)
        swap_loss = -lax.psum(part_loss, "data") / (2 * batch_total)
        grad_coef = 1.0 / (2 * batch_total * value_a11)
        grad_s_one = ((jnp.exp(logp_one) - codes_two) * grad_coef).astype(jnp.bfloat16)
        grad_s_two = ((jnp.exp(logp_two) - codes_one) * grad_coef).astype(jnp.bfloat16)
        dz_one = jnp.einsum("nk,kd->nd", grad_s_one, protos, preferred_element_type=jnp.float32)
        dz_two = jnp.einsum("nk,kd->nd", grad_s_two, protos, preferred_element_type=jnp.float32)
        proto_part = jnp.einsum("nk,nd->kd", grad_s_one, z_one, preferred_element_type=jnp.float32) + jnp.einsum("nk,nd->kd", grad_s_two, z_two, preferred_element_type=jnp.float32)
        grad_protos = lax.psum(proto_part, "data")
        return codes_one, codes_two, swap_loss, dz_one, dz_two, grad_protos

    row_spec = P("data", None)
    full_spec = P(None, None)
    return jax.shard_map(
        local_step,
        mesh=mesh,
        in_specs=(row_spec, row_spec, full_spec, row_spec, row_spec),
        out_specs=(row_spec, row_spec, P(), row_spec, row_spec, full_spec),
        check_vma=False,
    )
```

profile of v0, /device:TPU:0, one launch (start us, length us, event | category | flops | bytes accessed | tf_op | source)
XLA Modules:
  0.0 346.5 jit_solution(13428772911628497274)
XLA Ops:
  7.2 8.7 %fusion.11 = (f32[8192]{0:T(1024)}, f32[320,8192]{1,0:T(8,128)}) fusion(bf16[8192,256]{1,0:T(8,128)(2,1)} %param.8, bf16[256,256]{1,0:T(8,128)(2,1)} %param.10, bf16[64,256]{1,0:T(8,128)(2,1)} %param.7), kind=kOutput, calls=%fused_computation.20 | convolution fusion | flops 1347739648 | bytes 14876672 | tf_op jit(solution)/shard_map/nd,kd->nk/dot_general | solution.py:13
  16.0 6.2 %fusion.10 = (f32[8192]{0:T(1024)}, f32[320,8192]{1,0:T(8,128)}) fusion(bf16[8192,256]{1,0:T(8,128)(2,1)S(1)} %copy-done.1, bf16[256,256]{1,0:T(8,128)(2,1)S(1)} %copy-done.2, bf16[64,256]{1,0:T(8,128)(2,1)S(1)} %copy-done.3), kind=kOutput, calls=%fused_computation.19 | convolution fusion | flops 1347739648 | bytes 14876672 | tf_op jit(solution)/shard_map/nd,kd->nk/dot_general | solution.py:13
  24.3 2.1 exponential_reduce_fusion
  26.4 41.0 %all-reduce.14.cloned.1.call-done = (f32[8192]{0:T(1024)}, f32[8192]{0:T(1024)}) async-done(((f32[8192]{0:T(1024)}, f32[8192]{0:T(1024)}), (f32[8192]{0:T(1024)}, f32[8192]{0:T(1024)})) %all-reduce.14.cloned.1.call-update) | async-done | bytes 65552 | tf_op jit(solution)/shard_map/psum | solution.py:16
  68.3 6.2 %divide_reduce_fusion.1 = f32[320]{0:T(512)S(1)} fusion(f32[320,8192]{1,0:T(8,128)} %get-tuple-element.22, f32[8192]{0:T(1024)S(1)} %broadcast_multiply_fusion.5), kind=kLoop, calls=%fused_computation.14 | loop fusion | flops 7864000 | bytes 10519808 | tf_op jit(solution)/shard_map/reduce_sum | solution.py:18
  74.5 3.4 fusion.6
  78.0 2.0 divide_reduce_fusion
  80.0 3.4 fusion.7
  85.6 39.6 %all-reduce.12.cloned.1.call-done = (f32[8192]{0:T(1024)}, f32[8192]{0:T(1024)}) async-done(((f32[8192]{0:T(1024)}, f32[8192]{0:T(1024)}), (f32[8192]{0:T(1024)}, f32[8192]{0:T(1024)})) %all-reduce.12.cloned.1.call-update) | async-done | bytes 65552 | tf_op jit(solution)/shard_map/psum | solution.py:16
  125.9 7.0 %fusion.8 = f32[320]{0:T(512)S(1)} fusion(f32[320,8192]{1,0:T(8,128)} %get-tuple-element.24, f32[8192]{0:T(1024)S(1)} %broadcast_multiply_fusion.1, f32[320]{0:T(512)S(1)} %broadcast_multiply_fusion.7, f32[8192]{0:T(1024)S(1)} %broadcast_multiply_fusion.2), kind=kLoop, calls=%fused_computation.17 | loop fusion | flops 13106880 | bytes 10553856 | tf_op jit(solution)/shard_map/reduce_sum | solution.py:18
  132.9 7.1 %fusion.9 = f32[320]{0:T(512)S(1)} fusion(f32[320,8192]{1,0:T(8,128)} %get-tuple-element.22, f32[8192]{0:T(1024)S(1)} %broadcast_multiply_fusion.4, f32[320]{0:T(512)S(1)} %broadcast_multiply_fusion.9, f32[8192]{0:T(1024)S(1)} %broadcast_multiply_fusion.5), kind=kLoop, calls=%fused_computation.18 | loop fusion | flops 13106880 | bytes 10553856 | tf_op jit(solution)/shard_map/reduce_sum | solution.py:18
  140.0 14.2 %fusion.26 = (f32[8192]{0:T(1024)}, f32[320,8192]{1,0:T(8,128)}, f32[8192]{0:T(1024)}, f32[320,8192]{1,0:T(8,128)}) fusion(f32[320]{0:T(512)S(1)} %broadcast_multiply_fusion.6, f32[8192]{0:T(1024)S(1)} %broadcast_multiply_fusion.1, f32[320]{0:T(512)S(1)} %broadcast_multiply_fusion.7, f32[8192]{0:T(1024)S(1)} %broadcast_multiply_fusion.2, ...), kind=kLoop, calls=%fused_computation.57 | loop fusion | flops 31440896 | bytes 42144768 | tf_op jit(solution)/shard_map/reduce_sum | solution.py:19
  154.6 2.1 exponential_reduce_fusion.1
  156.7 39.3 %all-reduce.10.cloned.1.call-done = (f32[8192]{0:T(1024)}, f32[8192]{0:T(1024)}) async-done(((f32[8192]{0:T(1024)}, f32[8192]{0:T(1024)}), (f32[8192]{0:T(1024)}, f32[8192]{0:T(1024)})) %all-reduce.10.cloned.1.call-update) | async-done | bytes 65552 | tf_op jit(solution)/shard_map/psum | solution.py:19
  199.4 4.3 %multiply_convert_fusion.1 = (bf16[64,8192]{1,0:T(8,128)(2,1)S(1)}, f32[64,8192]{1,0:T(8,128)}) fusion(f32[320,8192]{1,0:T(8,128)} %get-tuple-element.22, f32[64]{0:T(128)S(1)} %log.9, f32[64]{0:T(128)S(1)} %fusion.12, f32[64]{0:T(128)S(1)} %divide_reduce_fusion.2, f32[8192]{0:T(1024)S(1)} %broadcast_multiply_fusion, f32[320,8192]{1,0:T(8,128)} %get-tuple-element.18), kind=kLoop, calls=%fused_computation.26 | loop fusion | flops 4194304 | bytes 7373568 | tf_op jit(solution)/shard_map/convert_element_type | solution.py:38
  206.9 4.3 %multiply_convert_fusion = (bf16[64,8192]{1,0:T(8,128)(2,1)S(1)}, f32[64,8192]{1,0:T(8,128)}) fusion(f32[320,8192]{1,0:T(8,128)} %get-tuple-element.24, f32[64]{0:T(128)S(1)} %log.10, f32[64]{0:T(128)S(1)} %fusion.14, f32[64]{0:T(128)S(1)} %divide_reduce_fusion.3, f32[8192]{0:T(1024)S(1)} %broadcast_multiply_fusion.3, f32[320,8192]{1,0:T(8,128)} %get-tuple-element.26), kind=kLoop, calls=%fused_computation.25 | loop fusion | flops 4194304 | bytes 7373568 | tf_op jit(solution)/shard_map/convert_element_type | solution.py:39
  211.3 4.7 %convolution_add_fusion = f32[8192,256]{1,0:T(8,128)} fusion(f32[8192,256]{1,0:T(8,128)S(1)} %fusion.32, bf16[64,8192]{1,0:T(8,128)(2,1)S(1)} %get-tuple-element.13, bf16[64,256]{1,0:T(8,128)(2,1)S(1)} %copy-done.4), kind=kOutput, calls=%fused_computation.8 | convolution fusion | flops 270532608 | bytes 17858560 | tf_op jit(solution)/shard_map/nk,nd->kd/dot_general | solution.py:42
  216.0 3.6 %multiply_reduce_fusion.1 = f32[]{:T(128)} fusion(f32[64,8192]{1,0:T(8,128)} %get-tuple-element.28, f32[320,8192]{1,0:T(8,128)} %get-tuple-element.22, f32[64]{0:T(128)S(1)} %log.9, f32[64]{0:T(128)S(1)} %fusion.12), kind=kLoop, calls=%fused_computation.28 | loop fusion | flops 2621439 | bytes 4194820 | tf_op jit(solution)/shard_map/reduce_sum | solution.py:35
  219.5 3.6 %multiply_reduce_fusion = f32[]{:T(128)} fusion(f32[64,8192]{1,0:T(8,128)} %get-tuple-element.27, f32[320,8192]{1,0:T(8,128)} %get-tuple-element.24, f32[64]{0:T(128)S(1)} %log.10, f32[64]{0:T(128)S(1)} %fusion.14), kind=kLoop, calls=%fused_computation.27 | loop fusion | flops 2621439 | bytes 4194820 | tf_op jit(solution)/shard_map/reduce_sum | solution.py:35
  224.4 22.9 %psum.62 = f32[]{:T(128)} all-reduce(f32[]{:T(128)S(6)} %add.22), channel_id=1, replica_groups=mesh['data'=8] {'data'}, use_global_device_ids=true, to_apply=%region_22.0 | all-reduce | flops 1 | bytes 8 | tf_op jit(solution)/shard_map/psum | solution.py:36
  248.0 3.6 %fusion.30 = f32[64,256]{1,0:T(8,128)} fusion(bf16[64,8192]{1,0:T(8,128)(2,1)S(1)} %get-tuple-element.15, bf16[8192,256]{1,0:T(8,128)(2,1)} %param.8), kind=kOutput, calls=%fused_computation.59 | convolution fusion | flops 268435456 | bytes 5308416 | tf_op jit(solution)/shard_map/nk,kd->nd/dot_general | solution.py:40
  251.6 3.6 %fusion.31 = f32[64,256]{1,0:T(8,128)} fusion(bf16[64,8192]{1,0:T(8,128)(2,1)S(1)} %get-tuple-element.13, bf16[8192,256]{1,0:T(8,128)(2,1)} %param.8), kind=kOutput, calls=%fused_computation.60 | convolution fusion | flops 268435456 | bytes 5308416 | tf_op jit(solution)/shard_map/nk,kd->nd/dot_general | solution.py:41
  255.2 76.3 %all-reduce.8.cloned.1.call-done = f32[8192,256]{1,0:T(8,128)} async-done(((f32[8192,256]{1,0:T(8,128)}), f32[8192,256]{1,0:T(8,128)}) %all-reduce.8.cloned.1.call-update) | async-done | bytes 8388624 | tf_op jit(solution)/shard_map/psum | solution.py:43
  331.5 7.3 %copy.18 = f32[8192,256]{1,0:T(8,128)} copy(f32[8192,256]{1,0:T(8,128)} %all-reduce.8.cloned.1.call-done) | data formatting | bytes 16777216
  (53 shorter events, 12.9 us)
Async XLA Ops:
  7.2 8.8 %copy-start.2 = (bf16[256,256]{1,0:T(8,128)(2,1)S(1)}, bf16[256,256]{1,0:T(8,128)(2,1)}, u32[]{:S(2)}) copy-start(bf16[256,256]{1,0:T(8,128)(2,1)} %param.9) | copy-start | bytes 393220
  7.2 8.8 %copy-start.3 = (bf16[64,256]{1,0:T(8,128)(2,1)S(1)}, bf16[64,256]{1,0:T(8,128)(2,1)}, u32[]{:S(2)}) copy-start(bf16[64,256]{1,0:T(8,128)(2,1)} %param.6) | copy-start | bytes 98308
  7.2 60.2 %all-reduce.14.cloned.1.call-start = ((), (), s32[]{:S(2)}) async-start(), calls=%async_computation.3 | async-start | bytes 131072 | tf_op jit(solution)/shard_map/psum | solution.py:16
  7.2 8.7 %copy-start.1 = (bf16[8192,256]{1,0:T(8,128)(2,1)S(1)}, bf16[8192,256]{1,0:T(8,128)(2,1)}, u32[]{:S(2)}) copy-start(bf16[8192,256]{1,0:T(8,128)(2,1)} %param.8) | copy-start | bytes 12582916
  22.2 102.9 %all-reduce.12.cloned.1.call-start = ((), (), s32[]{:S(2)}) async-start(), calls=%async_computation.2 | async-start | bytes 131072 | tf_op jit(solution)/shard_map/psum | solution.py:16
  67.4 7.1 %copy-start = (f32[320,8192]{1,0:T(8,128)S(1)}, f32[320,8192]{1,0:T(8,128)}, u32[]{:S(2)}) copy-start(f32[320,8192]{1,0:T(8,128)} %get-tuple-element.22) | copy-start | bytes 31457284
  68.3 9.7 %copy-start.5 = (f32[8192]{0:T(1024)S(1)}, f32[8192]{0:T(1024)}, u32[]{:S(2)}) copy-start(f32[8192]{0:T(1024)} %get-tuple-element.12) | copy-start | bytes 98308
  68.3 9.7 %slice-start = ((s8[10485760]{0:T(1024)(128)(4,1)}), s8[4194304]{0:T(1024)(128)(4,1)S(1)}, s32[]{:S(2)}) async-start(s8[10485760]{0:T(1024)(128)(4,1)} %bitcast.10), calls=%async_computation.4 | async-start | bytes 8388608
  68.3 9.7 %slice-start.1 = ((s8[10485760]{0:T(1024)(128)(4,1)}), s8[4194304]{0:T(1024)(128)(4,1)S(1)}, s32[]{:S(2)}) async-start(s8[10485760]{0:T(1024)(128)(4,1)} %bitcast.10), calls=%async_computation.5 | async-start | bytes 8388608
  74.5 3.5 slice-start.2
  83.5 112.6 %all-reduce.10.cloned.1.call-start = ((), (), s32[]{:S(2)}) async-start(), calls=%async_computation.1 | async-start | bytes 131072 | tf_op jit(solution)/shard_map/psum | solution.py:19
  125.1 7.7 %copy-start.6 = (f32[8192]{0:T(1024)S(1)}, f32[8192]{0:T(1024)}, u32[]{:S(2)}) copy-start(f32[8192]{0:T(1024)} %get-tuple-element.9) | copy-start | bytes 98308
  125.9 14.1 %slice-start.3 = ((s8[10485760]{0:T(1024)(128)(4,1)}), s8[4194304]{0:T(1024)(128)(4,1)S(1)}, s32[]{:S(2)}) async-start(s8[10485760]{0:T(1024)(128)(4,1)} %bitcast.12), calls=%async_computation.7 | async-start | bytes 8388608
  125.9 14.1 %slice-start.4 = ((s8[10485760]{0:T(1024)(128)(4,1)}), s8[4194304]{0:T(1024)(128)(4,1)S(1)}, s32[]{:S(2)}) async-start(s8[10485760]{0:T(1024)(128)(4,1)} %bitcast.12), calls=%async_computation.8 | async-start | bytes 8388608
  132.9 7.1 %slice-start.5 = ((s8[10485760]{0:T(1024)(128)(4,1)}), s8[2097152]{0:T(1024)(128)(4,1)S(1)}, s32[]{:S(2)}) async-start(s8[10485760]{0:T(1024)(128)(4,1)} %bitcast.12), calls=%async_computation.9 | async-start | bytes 4194304
  154.3 177.2 %all-reduce.8.cloned.1.call-start = ((), (), s32[]{:S(2)}) async-start(), calls=%async_computation | async-start | bytes 16777216 | tf_op jit(solution)/shard_map/psum | solution.py:43
  203.8 7.5 %copy-start.4 = (bf16[64,256]{1,0:T(8,128)(2,1)S(1)}, bf16[64,256]{1,0:T(8,128)(2,1)}, u32[]{:S(2)}) copy-start(bf16[64,256]{1,0:T(8,128)(2,1)} %param.7) | copy-start | bytes 98308
Sparse Core Ops, SparseCore 0:
  22.3 45.0 all-reduce.13
  83.6 41.5 all-reduce.11
  154.4 41.5 all-reduce.9
  216.1 115.3 all-reduce.7
where the time goes:
time: 347 us
  waiting for transfers between devices  196 us (56%)
  other arithmetic  73.9 us (21%)
  matrix products  28.1 us (8%)
  blocking collectives  22.9 us (7%)
  between operations  17 us (5%)
  local copies, waits for them, and re-layouts  7.38 us (2%)
    psum x3, waiting for transfers between devices, view_codes(): col_sum = lax.psum(jnp.sum(transport, axis=0), 'data')  120 us
    psum x1, waiting for transfers between devices, local_step(): grad_protos = lax.psum(proto_part, 'data')  76.3 us
    psum x1, blocking collectives, local_step(): swap_loss = -lax.psum(part_loss, 'data') / (2 * batch_total)  22.9 us
    reduce_sum x4, other arithmetic, view_codes(): jnp.sum(transport, axis=1, keepdims=True)  22.2 us
    reduce_sum x3, other arithmetic, view_codes(): col_sum = lax.psum(jnp.sum(transport, axis=0), 'data')  21.1 us
    dot_general x2, matrix products, view_codes(): jnp.einsum('nd,kd->nk', own_rows, protos, preferred_element_type=jnp.floa...  14.9 us
    unnamed x27, local copies, waits for them, and re-layouts  7.37 us
    reduce_sum x2, other arithmetic, local_step(): part_loss = jnp.sum(codes_two * logp_one) + jnp.sum(codes_one * logp_two)  7.12 us
  transfers between devices with their start and end apart: 4, of which 4 were waited for; matrix products, arithmetic and copies ran while one was open for 6% of the time, Pallas kernels for 0%

commit v1 on v0

v1 whole, which is shorter than its diff:
```python
import functools
import math

import jax
import jax.numpy as jnp
from jax import lax
from jax.experimental import pallas as pl
from jax.experimental.pallas import tpu as pltpu
from jax.sharding import PartitionSpec as P

MESH = pl.DeviceIdType.MESH
F32 = jnp.float32
BF16 = jnp.bfloat16
LOG2E = math.log2(math.e)
K20 = 20.0 * LOG2E
K10 = 10.0 * LOG2E
ITERS = 3
NB = 64
NQ = 256
NR = NB + NQ
D = 256
K = 8192
H = K // 2
TOTAL = 8 * NR
T = 512
NT = (((1,), (1,)), ((), ()))
NN = (((1,), (0,)), ((), ()))


def iota(shape, dim):
    return lax.broadcasted_iota(jnp.int32, shape, dim)


def sink_kernel(z1, z2, q1, q2, protos, za, c_out, nrm,
                ch, qp, xb, e, sb, cb, rb, arb, rsb, fb,
                load_sem, zs, zr, xs, xr, fs, fr, cs, cr, as_, ar, rs_, rr, ns, nr, ds_, dr):
    me = lax.axis_index("data")
    core = lax.rem(me, 2)
    chip = me // 2
    px = chip + 1 - 2 * lax.rem(chip, 2)
    py = lax.rem(chip + 2, 4)
    pd = 3 - chip
    peers = [px * 2 + core, py * 2 + core, pd * 2 + core]
    peer_chips = [px, py, pd]
    mate = me + 1 - 2 * core
    other = 1 - core

    loads = []
    for t in range(4):
        loads.append(pltpu.make_async_copy(
            protos.at[pl.ds(core * H + t * 1024, 1024)], ch.at[pl.ds(t * 1024, 1024)], load_sem.at[t]))
        loads[-1].start()

    bar = pltpu.get_barrier_semaphore()
    for dev in peers + [mate]:
        pl.semaphore_signal(bar, inc=1, device_id=(dev,), device_id_type=MESH)
    pl.semaphore_wait(bar, 4)

    def remote(src, dst, ssem, rsem, dev):
        return pltpu.make_async_remote_copy(src_ref=src, dst_ref=dst, send_sem=ssem, recv_sem=rsem,
                                            device_id=(dev,), device_id_type=MESH)

    zrows = pl.ds(pl.multiple_of(me * NB, NB), NB)
    sends = []
    zin = [z1, z2]
    qin = [q1, q2]
    for v in range(2):
        cp = remote(zin[v], za.at[v, zrows], xs.at[v], xr.at[v], mate)
        cp.start()
        sends.append(cp)
    for v in range(2):
        cp = remote(qin[v], qp.at[v], xs.at[2 + v], xr.at[2 + v], mate)
        cp.start()
        sends.append(cp)
    zcopies = []
    for p in range(3):
        for v in range(2):
            cp = remote(zin[v], za.at[v, zrows], zs.at[p, v], zr.at[p, v], peers[p])
            cp.start()
            zcopies.append(cp)

    for v in range(2):
        za[v, zrows, :] = zin[v][...]
        xb[core, v, 0:NB, :] = zin[v][...]
        xb[core, v, NB:NR, :] = qin[v][...]

    def score_block(c, first):
        def body(t, carry):
            cols = pl.ds(pl.multiple_of(t * T, T), T)
            ct = ch[cols, :]
            for v in range(2):
                s = lax.dot_general(xb[c, v], ct, NT, preferred_element_type=F32)
                ex = jnp.exp2(s * K20)
                e[v, pl.ds(pl.multiple_of(c * NR, NB), NR), cols] = ex
                sb[v, pl.ds(pl.multiple_of(c * NB, NB), NB), cols] = s[0:NB]
                col = jnp.sum(ex, axis=0, keepdims=True)
                if first:
                    arb[0, v, chip, :, cols] = col
                else:
                    arb[0, v, chip, :, cols] = arb[0, v, chip, :, cols] + col
            return carry
        return body

    per = H // T // 4
    for t in range(4):
        loads[t].wait()
        lax.fori_loop(t * per, (t + 1) * per, score_block(core, True), 0)

    for cp in sends:
        cp.wait_recv()
    mrows = pl.ds(pl.multiple_of(mate * NB, NB), NB)
    for v in range(2):
        xb[other, v, 0:NB, :] = za[v, mrows, :]
        xb[other, v, NB:NR, :] = qp[v]
    lax.fori_loop(0, H // T, score_block(other, False), 0)

    def send_cols(it, v):
        out = []
        for p in range(3):
            cp = remote(arb.at[it, v, chip], arb.at[it, v, chip], as_.at[it, v, p], ar.at[it, v, p], peers[p])
            cp.start()
            out.append(cp)
        return out

    flight = [send_cols(0, v) for v in range(2)]

    for cp in zcopies:
        cp.wait_recv()
    fwd = []
    for p in range(3):
        rows = pl.ds(pl.multiple_of(peers[p] * NB, NB), NB)
        for v in range(2):
            cp = remote(za.at[v, rows], za.at[v, rows], fs.at[p, v], fr.at[p, v], mate)
            cp.start()
            fwd.append(cp)

    ccopies = []

    def scale(it, v):
        for cp in flight[v]:
            cp.wait_recv()
        tot = (arb[it, v, 0] + arb[it, v, 1]) + (arb[it, v, 2] + arb[it, v, 3])
        cval = 1.0 / (K * tot)
        cb[v] = jnp.broadcast_to(cval, (8, H))
        if it == ITERS - 1:
            c_out[v, core] = cval
            cp = remote(c_out.at[v, core], c_out.at[v, core], cs.at[v], cr.at[v], mate)
            cp.start()
            ccopies.append(cp)

    lane8 = iota((8, 128), 1)
    sub8 = iota((8, 128), 0)

    def row_pass(it, v):
        def body(i, pack):
            accs = [jnp.zeros((8, 128), F32)] * 8
            for k in range(H // 128):
                ck = cb[v, :, k * 128:(k + 1) * 128]
                for g in range(8):
                    r0 = pl.multiple_of(i * 64 + g * 8, 8)
                    accs[g] = accs[g] + e[v, pl.ds(r0, 8), k * 128:(k + 1) * 128] * ck
            for g in range(8):
                rs = jnp.sum(accs[g], axis=1, keepdims=True)
                pack = jnp.where(lane8 == i * 8 + g, rs, pack)
            return pack
        pack = lax.fori_loop(0, 2 * NR // 64, body, jnp.zeros((8, 128), F32))
        rsb[it, v, core] = pack
        cp = remote(rsb.at[it, v, core], rsb.at[it, v, core], rs_.at[it, v], rr.at[it, v], mate)
        cp.start()
        return cp

    def col_pass(it, v, cp):
        cp.wait_recv()
        rtot = rsb[it, v, 0] + rsb[it, v, 1]
        r = 1.0 / (TOTAL * rtot)
        for g in range(2 * NR // 8):
            rb[v, g * 8:(g + 1) * 8, :] = jnp.broadcast_to(r[:, g:g + 1], (8, 128))
        for cc in range(4):
            def body(i, accs):
                accs = list(accs)
                for g in range(8):
                    r0 = pl.multiple_of(i * 64 + g * 8, 8)
                    rg = rb[v, pl.ds(r0, 8), :]
                    for k in range(8):
                        lo = cc * 1024 + k * 128
                        accs[k] = accs[k] + e[v, pl.ds(r0, 8), lo:lo + 128] * rg
                return tuple(accs)
            accs = lax.fori_loop(0, 2 * NR // 64, body, tuple(jnp.zeros((8, 128), F32) for _ in range(8)))
            for k in range(8):
                lo = cc * 1024 + k * 128
                arb[it + 1, v, chip, :, lo:lo + 128] = jnp.sum(accs[k], axis=0, keepdims=True)

    drain = []
    rcopies = []
    for it in range(ITERS - 1):
        cps = []
        for v in range(2):
            scale(it, v)
            cps.append(row_pass(it, v))
        drain += flight[0] + flight[1]
        rcopies += cps
        flight = [None, None]
        for v in range(2):
            col_pass(it, v, cps[v])
            flight[v] = send_cols(it + 1, v)

    def to_row(total, gg, col):
        return total + jnp.where(lane8 == gg * 8 + sub8, col, 0.0)

    def p_pass(v):
        def body(i, total):
            accs = [jnp.zeros((8, 128), F32)] * 8
            for k in range(H // 128):
                for g in range(8):
                    r0 = pl.multiple_of(i * 64 + g * 8, 8)
                    accs[g] = accs[g] + jnp.exp2(sb[v, pl.ds(r0, 8), k * 128:(k + 1) * 128] * K10)
            for g in range(8):
                total = to_row(total, i * 8 + g, jnp.sum(accs[g], axis=1, keepdims=True))
            return total
        total = lax.fori_loop(0, 2, body, jnp.zeros((8, 128), F32))
        fb[core, 4 + v:5 + v, :] = jnp.sum(total, axis=0, keepdims=True)

    def last_pass(v):
        def body(i, totals):
            tr, tl = totals
            for half in range(2):
                ra = [jnp.zeros((8, 128), F32)] * 4
                la = [jnp.zeros((8, 128), F32)] * 4
                for k in range(H // 128):
                    ck = cb[v, :, k * 128:(k + 1) * 128]
                    for g in range(4):
                        off = half * 32 + g * 8
                        re = pl.multiple_of(i * NR + off, 8)
                        rb_ = pl.multiple_of(i * NB + off, 8)
                        ec = e[v, pl.ds(re, 8), k * 128:(k + 1) * 128] * ck
                        ra[g] = ra[g] + ec
                        la[g] = la[g] + ec * sb[1 - v, pl.ds(rb_, 8), k * 128:(k + 1) * 128]
                for g in range(4):
                    gg = i * 8 + half * 4 + g
                    tr = to_row(tr, gg, jnp.sum(ra[g], axis=1, keepdims=True))
                    tl = to_row(tl, gg, jnp.sum(la[g], axis=1, keepdims=True))
            return tr, tl
        zero = jnp.zeros((8, 128), F32)
        tr, tl = lax.fori_loop(0, 2, body, (zero, zero))
        fb[core, v:v + 1, :] = jnp.sum(tr, axis=0, keepdims=True)
        fb[core, 2 + v:3 + v, :] = jnp.sum(tl, axis=0, keepdims=True)

    fb[core, 6:8, :] = jnp.zeros((2, 128), F32)
    for v in range(2):
        p_pass(v)
    for v in range(2):
        scale(ITERS - 1, v)
        last_pass(v)
    drain += flight[0] + flight[1]
    cp = remote(fb.at[core], fb.at[core], ds_, dr, mate)
    cp.start()
    cp.wait_recv()
    tot = fb[0] + fb[1]
    rinv = 1.0 / tot[0:2]
    pinv = 1.0 / tot[4:6]
    logp = jnp.log(tot[4:6])
    mean = tot[2:4] * rinv * 10.0
    loss = jnp.sum(mean - logp, axis=0, keepdims=True)
    nrm[chip, 0:2, :] = rinv
    nrm[chip, 2:4, :] = pinv
    nrm[chip, 4:5, :] = loss
    nrm[chip, 5:8, :] = jnp.zeros((3, 128), F32)
    ncopies = []
    for p in range(3):
        n = remote(nrm.at[chip], nrm.at[chip], ns.at[p], nr.at[p], peers[p])
        n.start()
        ncopies.append(n)
    cp.wait_send()
    for c in sends + zcopies + drain + rcopies:
        c.wait_send()
    for c in fwd + ccopies + ncopies:
        c.wait()


def sink_call(z1, z2, q1, q2, protos):
    vmem = pl.BlockSpec(memory_space=pltpu.VMEM)
    dma = pltpu.SemaphoreType.DMA
    return pl.pallas_call(
        sink_kernel,
        out_shape=(
            jax.ShapeDtypeStruct((2, 8 * NB, D), BF16),
            jax.ShapeDtypeStruct((2, 2, 1, H), F32),
            jax.ShapeDtypeStruct((4, 8, 128), F32),
        ),
        in_specs=[vmem] * 4 + [pl.BlockSpec(memory_space=pl.ANY)],
        out_specs=(vmem, vmem, vmem),
        scratch_shapes=[
            pltpu.VMEM((H, D), BF16),
            pltpu.VMEM((2, NQ, D), BF16),
            pltpu.VMEM((2, 2, NR, D), BF16),
            pltpu.VMEM((2, 2 * NR, H), F32),
            pltpu.VMEM((2, 2 * NB, H), F32),
            pltpu.VMEM((2, 8, H), F32),
            pltpu.VMEM((2, 2 * NR, 128), F32),
            pltpu.VMEM((ITERS, 2, 4, 1, H), F32),
            pltpu.VMEM((ITERS - 1, 2, 2, 8, 128), F32),
            pltpu.VMEM((2, 8, 128), F32),
            dma((4,)),
            dma((3, 2)), dma((3, 2)),
            dma((4,)), dma((4,)),
            dma((3, 2)), dma((3, 2)),
            dma((2,)), dma((2,)),
            dma((ITERS, 2, 3)), dma((ITERS, 2, 3)),
            dma((ITERS - 1, 2)), dma((ITERS - 1, 2)),
            dma((3,)), dma((3,)),
            dma, dma,
        ],
        compiler_params=pltpu.CompilerParams(collective_id=0, has_side_effects=True,
                                             vmem_limit_bytes=60 * 1024 * 1024),
        name="sink",
    )(z1, z2, q1, q2, protos)


TK = 512
COEF = 1.0 / (1024 * 0.1)


def grad_kernel(z1, z2, za, protos, c, nrm, codes1, codes2, dz1, dz2, gp, loss, own, prow):
    step = pl.program_id(0)

    @pl.when(step == 0)
    def _():
        me = lax.axis_index("data")
        core = lax.rem(me, 2)
        chip = me // 2
        mine = nrm[chip]
        pick = iota((NB, 128), 1) == iota((NB, 128), 0) + core * NB
        for q in range(4):
            col = jnp.sum(jnp.where(pick, jnp.broadcast_to(mine[q:q + 1], (NB, 128)), 0.0), axis=1, keepdims=True)
            own[q] = jnp.broadcast_to(col, (NB, 128))
            for d in range(4):
                prow[q, :, d * 128:(d + 1) * 128] = nrm[d, q:q + 1, :] * COEF
        tot = jnp.zeros((1, 128), F32)
        for d in range(4):
            tot = tot + nrm[d, 4:5, :]
        loss[...] = jnp.sum(tot, axis=1, keepdims=True) * (-1.0 / 1024)
        dz1[...] = jnp.zeros_like(dz1)
        dz2[...] = jnp.zeros_like(dz2)

    ct = protos[...]
    crow = [c[v] for v in range(2)]

    ex = []
    for z in (z1, z2):
        s = lax.dot_general(z[...], ct, NT, preferred_element_type=F32)
        ex.append(jnp.exp2(s * K10))
    code = []
    for v, out in enumerate((codes1, codes2)):
        q = ex[v] * ex[v] * crow[v] * own[v, :, 0:1]
        out[...] = q
        code.append(q)
    for v, dz in enumerate((dz1, dz2)):
        g = ((ex[v] * own[2 + v, :, 0:1] - code[1 - v]) * COEF).astype(BF16)
        dz[...] += lax.dot_general(g, ct, NN, preferred_element_type=F32)

    for b in range(TK // 128):
        rows = slice(b * 128, (b + 1) * 128)
        cb = ct[rows]
        et = []
        for v in range(2):
            s = lax.dot_general(cb, za[v], NT, preferred_element_type=F32)
            et.append(jnp.exp2(s * K10))
        acc = None
        for v in range(2):
            ccol = jnp.broadcast_to(crow[1 - v][:, b * 128:(b + 1) * 128], (128, 128)).T
            ccol = jnp.concatenate([ccol] * 4, axis=1)
            g = et[v] * prow[2 + v] - et[1 - v] * et[1 - v] * (ccol * prow[1 - v])
            part = lax.dot_general(g.astype(BF16), za[v], NN, preferred_element_type=F32)
            acc = part if acc is None else acc + part
        gp[rows, :] = acc


def grad_call(z1, z2, za, protos, c, nrm):
    full = lambda *shape: pl.BlockSpec(shape, lambda t: (0,) * len(shape))
    return pl.pallas_call(
        grad_kernel,
        grid=(K // TK,),
        out_shape=(
            jax.ShapeDtypeStruct((NB, K), F32),
            jax.ShapeDtypeStruct((NB, K), F32),
            jax.ShapeDtypeStruct((NB, D), F32),
            jax.ShapeDtypeStruct((NB, D), F32),
            jax.ShapeDtypeStruct((K, D), F32),
            jax.ShapeDtypeStruct((1, 1), F32),
        ),
        in_specs=[
            full(NB, D), full(NB, D), full(2, 8 * NB, D),
            pl.BlockSpec((TK, D), lambda t: (t, 0)),
            pl.BlockSpec((2, 1, TK), lambda t: (0, 0, t)),
            full(4, 8, 128),
        ],
        out_specs=(
            pl.BlockSpec((NB, TK), lambda t: (0, t)),
            pl.BlockSpec((NB, TK), lambda t: (0, t)),
            full(NB, D), full(NB, D),
            pl.BlockSpec((TK, D), lambda t: (t, 0)),
            full(1, 1),
        ),
        scratch_shapes=[pltpu.VMEM((4, NB, 128), F32), pltpu.VMEM((4, 1, 8 * NB), F32)],
        compiler_params=pltpu.CompilerParams(dimension_semantics=("arbitrary",)),
        name="grads",
    )(z1, z2, za, protos, c, nrm)


def solution(mesh):
    def local_step(z1, z2, protos, q1, q2):
        za, c, nrm = sink_call(z1, z2, q1, q2, protos)
        c = c.reshape(2, 1, K)
        codes1, codes2, dz1, dz2, gp, loss = grad_call(z1, z2, za, protos, c, nrm)
        return codes1, codes2, loss.reshape(()), dz1, dz2, gp

    row = P("data", None)
    full = P(None, None)
    return jax.shard_map(
        local_step,
        mesh=mesh,
        in_specs=(row, row, full, row, row),
        out_specs=(row, row, P(), row, row, full),
        check_vma=False,
    )
```

time: 347 us -> 72 us (0.21)
  waiting for transfers between devices: 196 us -> 0 us
  other arithmetic: 73.9 us -> 0 us
  Pallas kernels: 0 us -> 71.3 us
  matrix products: 28.1 us -> 0 us
  blocking collectives: 22.9 us -> 0 us
  between operations: 17 us -> 0.64 us
  local copies, waits for them, and re-layouts: 7.38 us -> 0 us
    psum x4 -> x0, waiting for transfers between devices: 196 us -> none  [the longest x3 120 us: view_codes(): col_sum = lax.psum(jnp.sum(transport, axis=0), 'data')]
    pallas_call x0 -> x2, Pallas kernels: none -> 71.3 us  [the longest x1 37.1 us: sink_call(): pl.pallas_call(sink_kernel, out_shape=(jax.ShapeDtypeStruct((2, 8 * NB, D...]
    reduce_sum x13 -> x0, other arithmetic: 58.4 us -> none  [the longest x4 22.2 us: view_codes(): jnp.sum(transport, axis=1, keepdims=True)]
    dot_general x6 -> x0, matrix products: 28.1 us -> none  [the longest x2 14.9 us: view_codes(): jnp.einsum('nd,kd->nk', own_rows, protos, preferred_element_type=jnp.floa...]
    psum x1 -> x0, blocking collectives: 22.9 us -> none  [local_step(): swap_loss = -lax.psum(part_loss, 'data') / (2 * batch_total)]
    convert_element_type x2 -> x0, other arithmetic: 8.66 us -> none  [the longest x1 4.33 us: local_step(): ((jnp.exp(logp_two) - codes_one) * grad_coef).astype(jnp.bfloat16)]
    unnamed x27 -> x0, local copies, waits for them, and re-layouts: 7.37 us -> none
    reduce_max x2 -> x0, other arithmetic: 3.65 us -> none  [the longest x1 1.83 us: local_step(): logp_one = jax.nn.log_softmax(score_one / value_a11, axis=1)]
  transfers between devices with their start and end apart: 4 -> 0, of which waited for: 4 -> 0; matrix products, arithmetic and copies ran while one was open for 6% -> 0% of each run, Pallas kernels for 0% -> 0%
where the time goes in v1:
time: 72 us; the launch traced here: 71.9 us
  Pallas kernels  71.3 us (99%)
    pallas_call x1, Pallas kernels, sink_call(): pl.pallas_call(sink_kernel, out_shape=(jax.ShapeDtypeStruct((2, 8 * NB, D...  37.1 us
    pallas_call x1, Pallas kernels, grad_call(): pl.pallas_call(grad_kernel, grid=(K // TK,), out_shape=(jax.ShapeDtypeStr...  34.2 us

profile of v1, /device:TPU:0, one launch (start us, length us, event | category | flops | bytes accessed | tf_op | source)
XLA Modules:
  0.0 71.9 jit_solution(13207408051188794245)
XLA Ops:
  0.6 37.1 %sink.1 = (bf16[2,512,256]{2,1,0:T(8,128)(2,1)}, f32[2,2,1,4096]{3,2,1,0:T(1,128)}, f32[4,8,128]{2,1,0:T(8,128)}) custom-call(bf16[64,256]{1,0:T(8,128)(2,1)} %z1.3, bf16[64,256]{1,0:T(8,128)(2,1)} %z2.3, bf16[256,256]{1,0:T(8,128)(2,1)} %q1.1, bf16[256,256]{1,0:T(8,128)(2,1)} %q2.1, bf16[8192,256]{1,0:T(8,128)(2,1)} %protos.3), custom_call_target="tpu_custom_call" | custom-call | tf_op jit(solution)/shard_map/sink/pallas_call | solution.py:283
  37.7 34.2 %grads.1 = (f32[64,8192]{1,0:T(8,128)}, f32[64,8192]{1,0:T(8,128)}, f32[64,256]{1,0:T(8,128)}, f32[64,256]{1,0:T(8,128)}, f32[8192,256]{1,0:T(8,128)}, /*index=5*/f32[1,1]{1,0:T(1,128)}) custom-call(bf16[64,256]{1,0:T(8,128)(2,1)} %z1.3, bf16[64,256]{1,0:T(8,128)(2,1)} %z2.3, bf16[2,512,256]{2,1,0:T(8,128)(2,1)} %get-tuple-element.15.za, ...), custom_call_target="tpu_custom_call" | custom-call | tf_op jit(solution)/shard_map/grads/pallas_call | solution.py:380

commit v2 on v1

--- a/solution.py
+++ b/solution.py
@@ -22,7 +22,7 @@
 K = 8192
 H = K // 2
 TOTAL = 8 * NR
-T = 512
+T = 1024
 NT = (((1,), (1,)), ((), ()))
 NN = (((1,), (0,)), ((), ()))
 
@@ -32,8 +32,8 @@
 
 
 def sink_kernel(z1, z2, q1, q2, protos, za, c_out, nrm,
-                ch, qp, xb, e, sb, cb, rb, arb, rsb, fb,
-                load_sem, zs, zr, xs, xr, fs, fr, cs, cr, as_, ar, rs_, rr, ns, nr, ds_, dr):
+                ch, xb, e, sb, cb, rb, arb, rsb, fb,
+                in_sem, load_sem, zs, zr, xs, xr, fs, fr, cs, cr, as_, ar, rs_, rr, ns, nr, ds_, dr):
     me = lax.axis_index("data")
     core = lax.rem(me, 2)
     chip = me // 2
@@ -45,6 +45,14 @@
     mate = me + 1 - 2 * core
     other = 1 - core
 
+    zrows = pl.ds(pl.multiple_of(me * NB, NB), NB)
+    rows_in = []
+    for v, (z, q) in enumerate(((z1, q1), (z2, q2))):
+        rows_in.append(pltpu.make_async_copy(z, xb.at[core, v, pl.ds(0, NB)], in_sem.at[v, 0]))
+        rows_in.append(pltpu.make_async_copy(q, xb.at[core, v, pl.ds(NB, NQ)], in_sem.at[v, 1]))
+        rows_in.append(pltpu.make_async_copy(z, za.at[v, zrows], in_sem.at[v, 2]))
+    for cp in rows_in:
+        cp.start()
     loads = []
     for t in range(4):
         loads.append(pltpu.make_async_copy(
@@ -54,35 +62,10 @@
     bar = pltpu.get_barrier_semaphore()
     for dev in peers + [mate]:
         pl.semaphore_signal(bar, inc=1, device_id=(dev,), device_id_type=MESH)
-    pl.semaphore_wait(bar, 4)
 
     def remote(src, dst, ssem, rsem, dev):
         return pltpu.make_async_remote_copy(src_ref=src, dst_ref=dst, send_sem=ssem, recv_sem=rsem,
                                             device_id=(dev,), device_id_type=MESH)
-
-    zrows = pl.ds(pl.multiple_of(me * NB, NB), NB)
-    sends = []
-    zin = [z1, z2]
-    qin = [q1, q2]
-    for v in range(2):
-        cp = remote(zin[v], za.at[v, zrows], xs.at[v], xr.at[v], mate)
-        cp.start()
-        sends.append(cp)
-    for v in range(2):
-        cp = remote(qin[v], qp.at[v], xs.at[2 + v], xr.at[2 + v], mate)
-        cp.start()
-        sends.append(cp)
-    zcopies = []
-    for p in range(3):
-        for v in range(2):
-            cp = remote(zin[v], za.at[v, zrows], zs.at[p, v], zr.at[p, v], peers[p])
-            cp.start()
-            zcopies.append(cp)
-
-    for v in range(2):
-        za[v, zrows, :] = zin[v][...]
-        xb[core, v, 0:NB, :] = zin[v][...]
-        xb[core, v, NB:NR, :] = qin[v][...]
 
     def score_block(c, first):
         def body(t, carry):
@@ -101,17 +84,31 @@
             return carry
         return body
 
-    per = H // T // 4
-    for t in range(4):
+    for cp in rows_in:
+        cp.wait()
+    loads[0].wait()
+    score_block(core, True)(0, 0)
+    pl.semaphore_wait(bar, 4)
+    sends = []
+    for v in range(2):
+        cp = remote(xb.at[core, v], xb.at[core, v], xs.at[v], xr.at[v], mate)
+        cp.start()
+        sends.append(cp)
+        cp = remote(za.at[v, zrows], za.at[v, zrows], xs.at[2 + v], xr.at[2 + v], mate)
+        cp.start()
+        sends.append(cp)
+    zcopies = []
+    for p in range(3):
+        for v in range(2):
+            cp = remote(za.at[v, zrows], za.at[v, zrows], zs.at[p, v], zr.at[p, v], peers[p])
+            cp.start()
+            zcopies.append(cp)
+    for t in range(1, 4):
         loads[t].wait()
-        lax.fori_loop(t * per, (t + 1) * per, score_block(core, True), 0)
+    lax.fori_loop(1, H // T, score_block(core, True), 0)
 
     for cp in sends:
         cp.wait_recv()
-    mrows = pl.ds(pl.multiple_of(mate * NB, NB), NB)
-    for v in range(2):
-        xb[other, v, 0:NB, :] = za[v, mrows, :]
-        xb[other, v, NB:NR, :] = qp[v]
     lax.fori_loop(0, H // T, score_block(other, False), 0)
 
     def send_cols(it, v):
@@ -154,11 +151,12 @@
     def row_pass(it, v):
         def body(i, pack):
             accs = [jnp.zeros((8, 128), F32)] * 8
-            for k in range(H // 128):
-                ck = cb[v, :, k * 128:(k + 1) * 128]
+            for kq in range(0, H // 128, 4):
+                ck = [cb[v, :, k * 128:(k + 1) * 128] for k in range(kq, kq + 4)]
                 for g in range(8):
                     r0 = pl.multiple_of(i * 64 + g * 8, 8)
-                    accs[g] = accs[g] + e[v, pl.ds(r0, 8), k * 128:(k + 1) * 128] * ck
+                    t = [e[v, pl.ds(r0, 8), (kq + j) * 128:(kq + j + 1) * 128] * ck[j] for j in range(4)]
+                    accs[g] = accs[g] + ((t[0] + t[1]) + (t[2] + t[3]))
             for g in range(8):
                 rs = jnp.sum(accs[g], axis=1, keepdims=True)
                 pack = jnp.where(lane8 == i * 8 + g, rs, pack)
@@ -210,10 +208,11 @@
     def p_pass(v):
         def body(i, total):
             accs = [jnp.zeros((8, 128), F32)] * 8
-            for k in range(H // 128):
+            for kq in range(0, H // 128, 4):
                 for g in range(8):
                     r0 = pl.multiple_of(i * 64 + g * 8, 8)
-                    accs[g] = accs[g] + jnp.exp2(sb[v, pl.ds(r0, 8), k * 128:(k + 1) * 128] * K10)
+                    t = [jnp.exp2(sb[v, pl.ds(r0, 8), (kq + j) * 128:(kq + j + 1) * 128] * K10) for j in range(4)]
+                    accs[g] = accs[g] + ((t[0] + t[1]) + (t[2] + t[3]))
             for g in range(8):
                 total = to_row(total, i * 8 + g, jnp.sum(accs[g], axis=1, keepdims=True))
             return total
@@ -226,15 +225,17 @@
             for half in range(2):
                 ra = [jnp.zeros((8, 128), F32)] * 4
                 la = [jnp.zeros((8, 128), F32)] * 4
-                for k in range(H // 128):
-                    ck = cb[v, :, k * 128:(k + 1) * 128]
+                for kq in range(0, H // 128, 4):
+                    ck = [cb[v, :, k * 128:(k + 1) * 128] for k in range(kq, kq + 4)]
                     for g in range(4):
                         off = half * 32 + g * 8
                         re = pl.multiple_of(i * NR + off, 8)
                         rb_ = pl.multiple_of(i * NB + off, 8)
-                        ec = e[v, pl.ds(re, 8), k * 128:(k + 1) * 128] * ck
-                        ra[g] = ra[g] + ec
-                        la[g] = la[g] + ec * sb[1 - v, pl.ds(rb_, 8), k * 128:(k + 1) * 128]
+                        lanes = [slice((kq + j) * 128, (kq + j + 1) * 128) for j in range(4)]
+                        t = [e[v, pl.ds(re, 8), lanes[j]] * ck[j] for j in range(4)]
+                        w = [t[j] * sb[1 - v, pl.ds(rb_, 8), lanes[j]] for j in range(4)]
+                        ra[g] = ra[g] + ((t[0] + t[1]) + (t[2] + t[3]))
+                        la[g] = la[g] + ((w[0] + w[1]) + (w[2] + w[3]))
                 for g in range(4):
                     gg = i * 8 + half * 4 + g
                     tr = to_row(tr, gg, jnp.sum(ra[g], axis=1, keepdims=True))
@@ -283,15 +284,14 @@
     return pl.pallas_call(
         sink_kernel,
         out_shape=(
-            jax.ShapeDtypeStruct((2, 8 * NB, D), BF16),
-            jax.ShapeDtypeStruct((2, 2, 1, H), F32),
-            jax.ShapeDtypeStruct((4, 8, 128), F32),
+            pltpu.VMEM((2, 8 * NB, D), BF16),
+            pltpu.VMEM((2, 2, 1, H), F32),
+            pltpu.VMEM((4, 8, 128), F32),
         ),
-        in_specs=[vmem] * 4 + [pl.BlockSpec(memory_space=pl.ANY)],
+        in_specs=[pl.BlockSpec(memory_space=pltpu.HBM)] * 5,
         out_specs=(vmem, vmem, vmem),
         scratch_shapes=[
             pltpu.VMEM((H, D), BF16),
-            pltpu.VMEM((2, NQ, D), BF16),
             pltpu.VMEM((2, 2, NR, D), BF16),
             pltpu.VMEM((2, 2 * NR, H), F32),
             pltpu.VMEM((2, 2 * NB, H), F32),
@@ -300,6 +300,7 @@
             pltpu.VMEM((ITERS, 2, 4, 1, H), F32),
             pltpu.VMEM((ITERS - 1, 2, 2, 8, 128), F32),
             pltpu.VMEM((2, 8, 128), F32),
+            dma((2, 3)),
             dma((4,)),
             dma((3, 2)), dma((3, 2)),
             dma((4,)), dma((4,)),
@@ -311,75 +312,153 @@
             dma, dma,
         ],
         compiler_params=pltpu.CompilerParams(collective_id=0, has_side_effects=True,
-                                             vmem_limit_bytes=60 * 1024 * 1024),
+                                             vmem_limit_bytes=50 * 1024 * 1024),
         name="sink",
     )(z1, z2, q1, q2, protos)
 
 
-TK = 512
+BK = 256
+NSUB = 4
+TK = NSUB * BK
+FIRST = 2 * TK
 COEF = 1.0 / (1024 * 0.1)
 
 
-def grad_kernel(z1, z2, za, protos, c, nrm, codes1, codes2, dz1, dz2, gp, loss, own, prow):
-    step = pl.program_id(0)
-
-    @pl.when(step == 0)
-    def _():
-        me = lax.axis_index("data")
-        core = lax.rem(me, 2)
-        chip = me // 2
-        mine = nrm[chip]
-        pick = iota((NB, 128), 1) == iota((NB, 128), 0) + core * NB
-        for q in range(4):
-            col = jnp.sum(jnp.where(pick, jnp.broadcast_to(mine[q:q + 1], (NB, 128)), 0.0), axis=1, keepdims=True)
-            own[q] = jnp.broadcast_to(col, (NB, 128))
-            for d in range(4):
-                prow[q, :, d * 128:(d + 1) * 128] = nrm[d, q:q + 1, :] * COEF
-        tot = jnp.zeros((1, 128), F32)
+def grad_kernel(za, protos, c, nrm, codes1, codes2, dz1, dz2, gp, loss,
+                ch, gst, cst, g0, g1, g2, g3, oscr, cc, own, prow, zat, z12, dz, lsem, gsem, csem):
+    la = pltpu.make_async_copy(protos.at[pl.ds(0, FIRST)], ch.at[pl.ds(0, FIRST)], lsem.at[0])
+    lb = pltpu.make_async_copy(protos.at[pl.ds(FIRST, K - FIRST)], ch.at[pl.ds(FIRST, K - FIRST)], lsem.at[1])
+    la.start()
+    lb.start()
+    me = lax.axis_index("data")
+    core = lax.rem(me, 2)
+    chip = me // 2
+    mine = nrm[chip]
+    pick = iota((NB, 128), 1) == iota((NB, 128), 0) + core * NB
+    for q in range(4):
+        col = jnp.sum(jnp.where(pick, jnp.broadcast_to(mine[q:q + 1], (NB, 128)), 0.0), axis=1, keepdims=True)
+        own[q] = jnp.broadcast_to(col, (NB, 128))
         for d in range(4):
-            tot = tot + nrm[d, 4:5, :]
-        loss[...] = jnp.sum(tot, axis=1, keepdims=True) * (-1.0 / 1024)
-        dz1[...] = jnp.zeros_like(dz1)
-        dz2[...] = jnp.zeros_like(dz2)
-
-    ct = protos[...]
-    crow = [c[v] for v in range(2)]
-
-    ex = []
-    for z in (z1, z2):
-        s = lax.dot_general(z[...], ct, NT, preferred_element_type=F32)
-        ex.append(jnp.exp2(s * K10))
-    code = []
-    for v, out in enumerate((codes1, codes2)):
-        q = ex[v] * ex[v] * crow[v] * own[v, :, 0:1]
-        out[...] = q
-        code.append(q)
-    for v, dz in enumerate((dz1, dz2)):
-        g = ((ex[v] * own[2 + v, :, 0:1] - code[1 - v]) * COEF).astype(BF16)
-        dz[...] += lax.dot_general(g, ct, NN, preferred_element_type=F32)
-
-    for b in range(TK // 128):
-        rows = slice(b * 128, (b + 1) * 128)
-        cb = ct[rows]
-        et = []
-        for v in range(2):
-            s = lax.dot_general(cb, za[v], NT, preferred_element_type=F32)
-            et.append(jnp.exp2(s * K10))
+            prow[q, d] = jnp.broadcast_to(nrm[d, q:q + 1, :] * COEF, (8, 128))
+    tot = jnp.zeros((1, 128), F32)
+    for d in range(4):
+        tot = tot + nrm[d, 4:5, :]
+    loss[...] = jnp.sum(tot, axis=1, keepdims=True) * (-1.0 / 1024)
+    for v in range(2):
+        z12[v * NB:(v + 1) * NB, :] = za[v, pl.ds(pl.multiple_of(me * NB, NB), NB), :]
+        zat[v] = za[v].T
+        g3[v] = jnp.zeros((4, BK, 128), BF16)
+    oscr[3] = jnp.zeros((2 * NB, BK), BF16)
+    dz[...] = jnp.zeros_like(dz)
+    codes = (codes1, codes2)
+    gs = (g0, g1, g2, g3)
+
+    def block(n):
+        return pl.ds(pl.multiple_of(n * BK, BK), BK)
+
+    def gradients(n, k):
         acc = None
         for v in range(2):
-            ccol = jnp.broadcast_to(crow[1 - v][:, b * 128:(b + 1) * 128], (128, 128)).T
-            ccol = jnp.concatenate([ccol] * 4, axis=1)
-            g = et[v] * prow[2 + v] - et[1 - v] * et[1 - v] * (ccol * prow[1 - v])
-            part = lax.dot_general(g.astype(BF16), za[v], NN, preferred_element_type=F32)
-            acc = part if acc is None else acc + part
-        gp[rows, :] = acc
-
-
-def grad_call(z1, z2, za, protos, c, nrm):
-    full = lambda *shape: pl.BlockSpec(shape, lambda t: (0,) * len(shape))
+            g = jnp.concatenate([gs[k][v, lt] for lt in range(4)], axis=1)
+            x = lax.dot_general(g, za[v], NN, preferred_element_type=F32)
+            acc = x if acc is None else acc + x
+        gst[block(n), :] = acc
+        dz[...] += lax.dot_general(oscr[k], ch[block(n), :], NN, preferred_element_type=F32)
+
+    def twice(x):
+        return jnp.concatenate([x, x], axis=0)
+
+    def pointwise(n, k):
+        ct = ch[block(n), :]
+        for rt in range(2):
+            s = [lax.dot_general(ct, zat[v, :, rt * 256:(rt + 1) * 256], NN, preferred_element_type=F32)
+                 for v in range(2)]
+            for b in range(BK // 16):
+                rows = slice(b * 16, (b + 1) * 16)
+                for l in range(2):
+                    lt = rt * 2 + l
+                    e = [jnp.exp2(s[v][rows, l * 128:(l + 1) * 128] * K10) for v in range(2)]
+                    u = [e[v] * e[v] * cc[v, k * BK + b * 16:k * BK + b * 16 + 16, :] for v in range(2)]
+                    for v in range(2):
+                        g = e[v] * twice(prow[2 + v, lt]) - u[1 - v] * twice(prow[1 - v, lt])
+                        gs[k][v, lt, rows, :] = g.astype(BF16)
+
+    def own_rows(n, k):
+        ct = ch[block(n), :]
+        s = lax.dot_general(z12[...], ct, NT, preferred_element_type=F32)
+        ex = jnp.exp2(s * K10)
+        ex = [ex[0:NB], ex[NB:2 * NB]]
+        code = []
+        for v in range(2):
+            q = ex[v] * ex[v] * c[v, :, block(n)] * own[v, :, 0:1]
+            cst[v, :, block(n)] = q
+            code.append(q)
+        for v in range(2):
+            g = (ex[v] * own[2 + v, :, 0:1] - code[1 - v]) * COEF
+            oscr[k, v * NB:(v + 1) * NB, :] = g.astype(BF16)
+
+    def gcopy(j):
+        rows = pl.ds(pl.multiple_of(j * TK, TK), TK)
+        return pltpu.make_async_copy(gst.at[rows], gp.at[rows], gsem.at[j])
+
+    def ccopy(v, j):
+        cols = pl.ds(pl.multiple_of(j * TK, TK), TK)
+        return pltpu.make_async_copy(cst.at[v, :, cols], codes[v].at[:, cols], csem.at[v, j])
+
+    def body(m, carry):
+        @pl.when(m >= 1)
+        def _():
+            ccopy(0, m - 1).start()
+            ccopy(1, m - 1).start()
+
+        @pl.when(m >= 2)
+        def _():
+            gcopy(m - 2).start()
+
+        n = NSUB * m
+        for v in range(2):
+            crow = c[v, :, pl.ds(pl.multiple_of(m * TK, TK), TK)]
+            for b in range(TK // 128):
+                cc[v, b * 128:(b + 1) * 128, :] = jnp.broadcast_to(crow[:, b * 128:(b + 1) * 128], (128, 128)).T
+        for k in range(NSUB):
+            pointwise(n + k, k)
+            own_rows(n + k, k)
+            if k == 0:
+                gradients(jnp.maximum(n - 1, 0), NSUB - 1)
+            else:
+                gradients(n + k - 1, k - 1)
+        return carry
+
+    la.wait()
+    lax.fori_loop(0, 2, body, 0)
+    lb.wait()
+    groups = K // TK
+    lax.fori_loop(2, groups, body, 0)
+    ccopy(0, groups - 1).start()
+    ccopy(1, groups - 1).start()
+    gcopy(groups - 2).start()
+    gradients(K // BK - 1, NSUB - 1)
+    gcopy(groups - 1).start()
+    dz1[...] = dz[0:NB]
+    dz2[...] = dz[NB:2 * NB]
+
+    def drain(j, carry):
+        gcopy(j).wait()
+        ccopy(0, j).wait()
+        ccopy(1, j).wait()
+        return carry
+
+    lax.fori_loop(0, groups, drain, 0)
+
+
+def grad_call(za, protos, c, nrm):
+    vmem = pl.BlockSpec(memory_space=pltpu.VMEM)
+    hbm = pl.BlockSpec(memory_space=pl.ANY)
+    pin = pl.BlockSpec(memory_space=pltpu.HBM)
+    dma = pltpu.SemaphoreType.DMA
+    gscr = pltpu.VMEM((2, 4, BK, 128), BF16)
     return pl.pallas_call(
         grad_kernel,
-        grid=(K // TK,),
         out_shape=(
             jax.ShapeDtypeStruct((NB, K), F32),
             jax.ShapeDtypeStruct((NB, K), F32),
@@ -388,30 +467,33 @@
             jax.ShapeDtypeStruct((K, D), F32),
             jax.ShapeDtypeStruct((1, 1), F32),
         ),
-        in_specs=[
-            full(NB, D), full(NB, D), full(2, 8 * NB, D),
-            pl.BlockSpec((TK, D), lambda t: (t, 0)),
-            pl.BlockSpec((2, 1, TK), lambda t: (0, 0, t)),
-            full(4, 8, 128),
+        in_specs=[vmem, pin, vmem, vmem],
+        out_specs=(hbm, hbm, vmem, vmem, hbm, vmem),
+        scratch_shapes=[
+            pltpu.VMEM((K, D), BF16),
+            pltpu.VMEM((K, D), F32),
+            pltpu.VMEM((2, NB, K), F32),
+            gscr, gscr, gscr, gscr,
+            pltpu.VMEM((NSUB, 2 * NB, BK), BF16),
+            pltpu.VMEM((2, TK, 128), F32),
+            pltpu.VMEM((4, NB, 128), F32),
+            pltpu.VMEM((4, 4, 8, 128), F32),
+            pltpu.VMEM((2, D, 8 * NB), BF16),
+            pltpu.VMEM((2 * NB, D), BF16),
+            pltpu.VMEM((2 * NB, D), F32),
+            dma((2,)), dma((K // TK,)), dma((2, K // TK)),
         ],
-        out_specs=(
-            pl.BlockSpec((NB, TK), lambda t: (0, t)),
-            pl.BlockSpec((NB, TK), lambda t: (0, t)),
-            full(NB, D), full(NB, D),
-            pl.BlockSpec((TK, D), lambda t: (t, 0)),
-            full(1, 1),
-        ),
-        scratch_shapes=[pltpu.VMEM((4, NB, 128), F32), pltpu.VMEM((4, 1, 8 * NB), F32)],
-        compiler_params=pltpu.CompilerParams(dimension_semantics=("arbitrary",)),
+        compiler_params=pltpu.CompilerParams(vmem_limit_bytes=50 * 1024 * 1024),
         name="grads",
-    )(z1, z2, za, protos, c, nrm)
+    )(za, protos, c, nrm)
 
 
 def solution(mesh):
     def local_step(z1, z2, protos, q1, q2):
+        z1, z2, q1, q2, protos = (pltpu.with_memory_space_constraint(x, pltpu.HBM) for x in (z1, z2, q1, q2, protos))
         za, c, nrm = sink_call(z1, z2, q1, q2, protos)
         c = c.reshape(2, 1, K)
-        codes1, codes2, dz1, dz2, gp, loss = grad_call(z1, z2, za, protos, c, nrm)
+        codes1, codes2, dz1, dz2, gp, loss = grad_call(za, protos, c, nrm)
         return codes1, codes2, loss.reshape(()), dz1, dz2, gp
 
     row = P("data", None)

time: 72 us -> 49.8 us (0.69)
  Pallas kernels: 71.3 us -> 49 us
    pallas_call x2, Pallas kernels: 71.3 us -> 49 us  [the longest x1 32.3 us: sink_call(): pl.pallas_call(sink_kernel, out_shape=(pltpu.VMEM((2, 8 * NB, D), BF16),...]
where the time goes in v2:
time: 49.8 us; the launch traced here: 49.7 us
  Pallas kernels  49 us (98%)
  between operations  0.64 us (1%)
    pallas_call x1, Pallas kernels, sink_call(): pl.pallas_call(sink_kernel, out_shape=(pltpu.VMEM((2, 8 * NB, D), BF16),...  32.3 us
    pallas_call x1, Pallas kernels, grad_call(): pl.pallas_call(grad_kernel, out_shape=(jax.ShapeDtypeStruct((NB, K), F32)...  16.7 us

profile of v2, /device:TPU:0, one launch (start us, length us, event | category | flops | bytes accessed | tf_op | source)
XLA Modules:
  0.0 49.7 jit_solution(14491302131581525546)
XLA Ops:
  0.6 32.3 %sink.1 = (bf16[2,512,256]{2,1,0:T(8,128)(2,1)S(1)}, f32[2,2,1,4096]{3,2,1,0:T(1,128)S(1)}, f32[4,8,128]{2,1,0:T(8,128)S(1)}) custom-call(bf16[64,256]{1,0:T(8,128)(2,1)} %z1.1, bf16[64,256]{1,0:T(8,128)(2,1)} %z2.1, bf16[256,256]{1,0:T(8,128)(2,1)} %q1.1, bf16[256,256]{1,0:T(8,128)(2,1)} %q2.1, bf16[8192,256]{1,0:T(8,128)(2,1)} %protos.3), custom_call_target="tpu_custom_call" | custom-call | tf_op jit(solution)/shard_map/sink/pallas_call | solution.py:284
  33.0 16.7 %grads.1 = (f32[64,8192]{1,0:T(8,128)}, f32[64,8192]{1,0:T(8,128)}, f32[64,256]{1,0:T(8,128)}, f32[64,256]{1,0:T(8,128)}, f32[8192,256]{1,0:T(8,128)}, /*index=5*/f32[1,1]{1,0:T(1,128)}) custom-call(bf16[2,512,256]{2,1,0:T(8,128)(2,1)S(1)} %get-tuple-element.15.za, bf16[8192,256]{1,0:T(8,128)(2,1)} %protos.3, f32[2,1,8192]{2,1,0:T(1,128)S(1)} %bitcast.2, ...), custom_call_target="tpu_custom_call" | custom-call | tf_op jit(solution)/shard_map/grads/pallas_call | solution.py:460

commit v3 on v2

--- a/solution.py
+++ b/solution.py
@@ -40,8 +40,7 @@
     px = chip + 1 - 2 * lax.rem(chip, 2)
     py = lax.rem(chip + 2, 4)
     pd = 3 - chip
-    peers = [px * 2 + core, py * 2 + core, pd * 2 + core]
-    peer_chips = [px, py, pd]
+    peers = [pd * 2 + core, px * 2 + core, py * 2 + core]
     mate = me + 1 - 2 * core
     other = 1 - core
 
@@ -150,18 +149,18 @@
 
     def row_pass(it, v):
         def body(i, pack):
-            accs = [jnp.zeros((8, 128), F32)] * 8
+            accs = [jnp.zeros((8, 128), F32)] * 16
             for kq in range(0, H // 128, 4):
                 ck = [cb[v, :, k * 128:(k + 1) * 128] for k in range(kq, kq + 4)]
-                for g in range(8):
-                    r0 = pl.multiple_of(i * 64 + g * 8, 8)
+                for g in range(16):
+                    r0 = pl.multiple_of(i * 128 + g * 8, 8)
                     t = [e[v, pl.ds(r0, 8), (kq + j) * 128:(kq + j + 1) * 128] * ck[j] for j in range(4)]
                     accs[g] = accs[g] + ((t[0] + t[1]) + (t[2] + t[3]))
-            for g in range(8):
+            for g in range(16):
                 rs = jnp.sum(accs[g], axis=1, keepdims=True)
-                pack = jnp.where(lane8 == i * 8 + g, rs, pack)
+                pack = jnp.where(lane8 == i * 16 + g, rs, pack)
             return pack
-        pack = lax.fori_loop(0, 2 * NR // 64, body, jnp.zeros((8, 128), F32))
+        pack = lax.fori_loop(0, 2 * NR // 128, body, jnp.zeros((8, 128), F32))
         rsb[it, v, core] = pack
         cp = remote(rsb.at[it, v, core], rsb.at[it, v, core], rs_.at[it, v], rr.at[it, v], mate)
         cp.start()
@@ -176,14 +175,14 @@
         for cc in range(4):
             def body(i, accs):
                 accs = list(accs)
-                for g in range(8):
-                    r0 = pl.multiple_of(i * 64 + g * 8, 8)
+                for g in range(16):
+                    r0 = pl.multiple_of(i * 128 + g * 8, 8)
                     rg = rb[v, pl.ds(r0, 8), :]
                     for k in range(8):
                         lo = cc * 1024 + k * 128
                         accs[k] = accs[k] + e[v, pl.ds(r0, 8), lo:lo + 128] * rg
                 return tuple(accs)
-            accs = lax.fori_loop(0, 2 * NR // 64, body, tuple(jnp.zeros((8, 128), F32) for _ in range(8)))
+            accs = lax.fori_loop(0, 2 * NR // 128, body, tuple(jnp.zeros((8, 128), F32) for _ in range(8)))
             for k in range(8):
                 lo = cc * 1024 + k * 128
                 arb[it + 1, v, chip, :, lo:lo + 128] = jnp.sum(accs[k], axis=0, keepdims=True)

time: 49.8 us -> 47.4 us (0.952)
  Pallas kernels: 49 us -> 46.6 us
    pallas_call x1, Pallas kernels: 32.3 us -> 29.9 us  [sink_call(): pl.pallas_call(sink_kernel, out_shape=(pltpu.VMEM((2, 8 * NB, D), BF16),...]
where the time goes in v3:
time: 47.4 us; the launch traced here: 47.3 us
  Pallas kernels  46.6 us (98%)
  between operations  0.64 us (1%)
    pallas_call x1, Pallas kernels, sink_call(): pl.pallas_call(sink_kernel, out_shape=(pltpu.VMEM((2, 8 * NB, D), BF16),...  29.9 us
    pallas_call x1, Pallas kernels, grad_call(): pl.pallas_call(grad_kernel, out_shape=(jax.ShapeDtypeStruct((NB, K), F32)...  16.7 us

profile of v3, /device:TPU:0, one launch (start us, length us, event | category | flops | bytes accessed | tf_op | source)
XLA Modules:
  0.0 47.3 jit_solution(13769381419857737499)
XLA Ops:
  0.6 29.9 %sink.1 = (bf16[2,512,256]{2,1,0:T(8,128)(2,1)S(1)}, f32[2,2,1,4096]{3,2,1,0:T(1,128)S(1)}, f32[4,8,128]{2,1,0:T(8,128)S(1)}) custom-call(bf16[64,256]{1,0:T(8,128)(2,1)} %z1.1, bf16[64,256]{1,0:T(8,128)(2,1)} %z2.1, bf16[256,256]{1,0:T(8,128)(2,1)} %q1.1, bf16[256,256]{1,0:T(8,128)(2,1)} %q2.1, bf16[8192,256]{1,0:T(8,128)(2,1)} %protos.3), custom_call_target="tpu_custom_call" | custom-call | tf_op jit(solution)/shard_map/sink/pallas_call | solution.py:283
  30.6 16.7 %grads.1 = (f32[64,8192]{1,0:T(8,128)}, f32[64,8192]{1,0:T(8,128)}, f32[64,256]{1,0:T(8,128)}, f32[64,256]{1,0:T(8,128)}, f32[8192,256]{1,0:T(8,128)}, /*index=5*/f32[1,1]{1,0:T(1,128)}) custom-call(bf16[2,512,256]{2,1,0:T(8,128)(2,1)S(1)} %get-tuple-element.15.za, bf16[8192,256]{1,0:T(8,128)(2,1)} %protos.3, f32[2,1,8192]{2,1,0:T(1,128)S(1)} %bitcast.2, ...), custom_call_target="tpu_custom_call" | custom-call | tf_op jit(solution)/shard_map/grads/pallas_call | solution.py:459
